TPU v7x, 32 devices: a whole 2x2x4 slice. The times are simulated.
32 devices in a mesh: farcp: 4 (over x, core), nearcp: 2 (over y), heads: 4 (over z).
Axes of the slice: x: 2, y: 2, z: 4, core: 2. Of those that a mesh axis runs over, the one named last changes fastest.
Arguments:
- raw_keys: bfloat16 [8, 2048, 8, 128], P(None, ('farcp', 'nearcp'), 'heads'), may hold values from -6 to 6
- raw_values: bfloat16 [8, 2048, 8, 128], P(None, ('farcp', 'nearcp'), 'heads'), may hold values from -6 to 6
- turn_angle: float32 [2048, 64], replicated, may hold values from -3.140625 to 3.140625
- key_gain: float32 [128], replicated, may hold values from 0.25 to 1.75
Outputs:
- cache_keys: bfloat16 [8, 2048, 8, 128], P(('farcp', 'nearcp'), None, 'heads')
- cache_values: bfloat16 [8, 2048, 8, 128], P(('farcp', 'nearcp'), None, 'heads')
- key_scale: float32 [8, 8, 128], P(('farcp', 'nearcp'), 'heads')
All inputs are finite; a program needn't handle non-finite values. Where the computation divides by a largest or mean magnitude, that divisor is 1e-20 or more.
Results may differ from a plain program's by a relative error of at most 0.001.
Values may be sent and summed in bfloat16 or wider, within the bound.
No kernel may reach another device: no remote copies, remote signals or barrier semaphores. Data moves between devices by JAX's collectives and lax.ppermute only.
A program may use at most 128 MiB of HBM per device.

v0:
```python
import jax
import jax.numpy as jnp
from jax import lax
from jax.sharding import PartitionSpec as P


def turn_pairs(vectors, angle):
    half = vectors.shape[-1] // 2
    cosine, sine = (jnp.cos(angle)[None, :, None, :], jnp.sin(angle)[None, :, None, :])
    first, second = (vectors[..., :half], vectors[..., half:])
    return jnp.concatenate(
        [first * cosine - second * sine, second * cosine + first * sine], axis=-1
    )


def unit_rows(vectors, row_gain):
    return (
        vectors * lax.rsqrt(jnp.mean(vectors * vectors, axis=-1, keepdims=True) + 1e-06) * row_gain
    )


def ready_to_store(plain_keys, angle, key_gain):
    wide_keys = plain_keys.astype(jnp.float32)
    wide_keys = unit_rows(wide_keys, key_gain)
    return turn_pairs(wide_keys, angle)


def shards(raw_keys, raw_values, turn_angle, key_gain):
    moved_keys, cache_values = (
        lax.all_to_all(raw_keys, ("farcp", "nearcp"), split_axis=0, concat_axis=1, tiled=True),
        lax.all_to_all(raw_values, ("farcp", "nearcp"), split_axis=0, concat_axis=1, tiled=True),
    )
    turned_keys = ready_to_store(moved_keys, turn_angle, key_gain)
    key_scale = jnp.max(jnp.abs(turned_keys), axis=1)
    narrow_keys = (turned_keys / key_scale[:, None]).astype(jnp.bfloat16)
    return (narrow_keys, cache_values, key_scale)


def solution(mesh):
    in_specs = (
        P(None, ("farcp", "nearcp"), "heads", None),
        P(None, ("farcp", "nearcp"), "heads", None),
        P(),
        P(),
    )
    out_specs = (
        P(("farcp", "nearcp"), None, "heads", None),
        P(("farcp", "nearcp"), None, "heads", None),
        P(("farcp", "nearcp"), "heads", None),
    )
    return jax.shard_map(shards, mesh=mesh, in_specs=in_specs, out_specs=out_specs, check_vma=False)
```

profile of v0, /device:TPU:0, one launch (start us, length us, event | category | flops | bytes accessed | tf_op | source)
XLA Modules:
  0.0 47.4 jit_solution(12344306644304988515)
XLA Ops:
  0.6 0.0 copy-start
  0.6 5.3 %all-to-all-start = ((bf16[8,256,2,128]{3,2,1,0:T(2,128)(2,1)}), bf16[8,256,2,128]{3,2,1,0:T(2,128)(2,1)S(1)}, u32[]{:S(2)}, u32[]{:S(2)}) async-start(bf16[8,256,2,128]{3,2,1,0:T(2,128)(2,1)} %param.4), calls=%async_computation | async-start | bytes 2097152 | tf_op jit(solution)/shard_map/all_to_all | solution.py:30
  6.0 0.0 copy-done
  6.0 2.6 %fusion.1 = (f32[2048,64]{0,1:T(8,128)S(1)}, f32[2048,64]{0,1:T(8,128)}) fusion(f32[2048,64]{0,1:T(8,128)S(1)} %copy-done), kind=kLoop, calls=%fused_computation.9 | loop fusion | bytes 1572864 | tf_op jit(solution)/shard_map/cos | solution.py:9
  8.5 0.3 copy.7
  8.9 1.4 %copy.8 = f32[2048,64]{1,0:T(8,128)S(1)} copy(f32[2048,64]{0,1:T(8,128)} %get-tuple-element.6) | data formatting | bytes 1048576 | tf_op jit(solution)/shard_map/sin | solution.py:9
  10.3 10.2 %all-to-all-done = bf16[8,256,2,128]{3,2,1,0:T(2,128)(2,1)S(1)} async-done(((bf16[8,256,2,128]{3,2,1,0:T(2,128)(2,1)}), bf16[8,256,2,128]{3,2,1,0:T(2,128)(2,1)S(1)}, u32[]{:S(2)}, u32[]{:S(2)}) %all-to-all-start) | async-done | bytes 1048608 | tf_op jit(solution)/shard_map/all_to_all | solution.py:30
  20.5 4.2 %all-to-all-start.1 = ((bf16[8,256,2,128]{3,2,1,0:T(2,128)(2,1)}), bf16[8,256,2,128]{3,2,1,0:T(2,128)(2,1)}, u32[]{:S(2)}, u32[]{:S(2)}) async-start(bf16[8,256,2,128]{3,2,1,0:T(2,128)(2,1)} %param.5), calls=%async_computation.1 | async-start | bytes 2097152 | tf_op jit(solution)/shard_map/all_to_all | solution.py:31
  24.8 2.3 %multiply_reduce_fusion = f32[8,256,2]{2,1,0:T(8,128)S(1)} fusion(bf16[8,256,2,128]{3,2,1,0:T(2,128)(2,1)S(1)} %all-to-all-done), kind=kLoop, calls=%fused_computation.6 | loop fusion | flops 1568768 | bytes 1064960 | tf_op jit(solution)/shard_map/reduce_sum | solution.py:18
  27.0 0.1 add_rsqrt_fusion
  27.2 0.0 copy-start.2
  27.2 0.7 %convert_element_type.34 = f32[8,256,2,128]{3,2,1,0:T(2,128)S(1)} convert(bf16[8,256,2,128]{3,2,1,0:T(2,128)(2,1)S(1)} %all-to-all-done) | non-fusion elementwise | flops 524288 | bytes 3145728 | tf_op jit(solution)/shard_map/convert_element_type | solution.py:23
  27.9 0.0 copy-done.2
  27.9 4.8 %fusion = f32[1,2048,2,128]{3,2,1,0:T(2,128)S(1)} fusion(f32[128]{0:T(128)S(1)} %copy-done.2, f32[2048,2]{1,0:T(8,128)S(1)} %bitcast.9, f32[1,2048,2,128]{3,2,1,0:T(2,128)S(1)} %bitcast.8), kind=kLoop, calls=%fused_computation.2 | loop fusion | flops 1048576 | bytes 4211200 | tf_op jit(solution)/shard_map/mul | solution.py:18
  32.8 6.3 %multiply_subtract_fusion = (f32[1,2048,2,64]{3,2,1,0:T(2,128)S(1)}, f32[1,2048,2,64]{3,2,1,0:T(2,128)S(1)}) fusion(f32[1,2048,2,128]{3,2,1,0:T(2,128)S(1)} %fusion, f32[2048,64]{1,0:T(8,128)S(1)} %copy.8, f32[2048,64]{1,0:T(8,128)S(1)} %copy.7), kind=kLoop, calls=%fused_computation.5 | loop fusion | flops 1572864 | bytes 5242880 | tf_op jit(solution)/shard_map/sub | solution.py:12
  39.1 2.6 %abs_reduce_fusion = f32[2,128]{1,0:T(2,128)S(1)} fusion(f32[1,2048,2,64]{3,2,1,0:T(2,128)S(1)} %get-tuple-element.4, f32[1,2048,2,64]{3,2,1,0:T(2,128)S(1)} %get-tuple-element.3), kind=kLoop, calls=%fused_computation.3 | loop fusion | flops 1572608 | bytes 2098176 | tf_op jit(solution)/shard_map/reduce_max | solution.py:34
  41.7 0.0 copy-start.1
  41.7 3.1 %divide_convert_fusion = bf16[1,2048,2,128]{3,2,1,0:T(2,128)(2,1)} fusion(f32[2,128]{1,0:T(2,128)S(1)} %abs_reduce_fusion, f32[1,2048,2,64]{3,2,1,0:T(2,128)S(1)} %get-tuple-element.4, f32[1,2048,2,64]{3,2,1,0:T(2,128)S(1)} %get-tuple-element.3), kind=kLoop, calls=%fused_computation.7 | loop fusion | flops 1572864 | bytes 3146752 | tf_op jit(solution)/shard_map/convert_element_type | solution.py:35
  44.8 0.0 copy-done.1
  44.8 0.0 all-to-all-done.1
  44.8 2.6 %copy.10 = bf16[1,2048,2,128]{3,2,1,0:T(2,128)(2,1)} copy(bf16[1,2048,2,128]{3,2,1,0:T(2,128)(2,1)} %bitcast.2) | data formatting | bytes 2097152
Async XLA Ops:
  0.6 5.4 %copy-start = (f32[2048,64]{0,1:T(8,128)S(1)}, f32[2048,64]{0,1:T(8,128)}, u32[]{:S(2)}) copy-start(f32[2048,64]{0,1:T(8,128)} %param.6) | copy-start | bytes 1572868
  0.6 19.9 %all-to-all-start = ((bf16[8,256,2,128]{3,2,1,0:T(2,128)(2,1)}), bf16[8,256,2,128]{3,2,1,0:T(2,128)(2,1)S(1)}, u32[]{:S(2)}, u32[]{:S(2)}) async-start(bf16[8,256,2,128]{3,2,1,0:T(2,128)(2,1)} %param.4), calls=%async_computation | async-start | bytes 2097152 | tf_op jit(solution)/shard_map/all_to_all | solution.py:30
  20.5 24.3 %all-to-all-start.1 = ((bf16[8,256,2,128]{3,2,1,0:T(2,128)(2,1)}), bf16[8,256,2,128]{3,2,1,0:T(2,128)(2,1)}, u32[]{:S(2)}, u32[]{:S(2)}) async-start(bf16[8,256,2,128]{3,2,1,0:T(2,128)(2,1)} %param.5), calls=%async_computation.1 | async-start | bytes 2097152 | tf_op jit(solution)/shard_map/all_to_all | solution.py:31
  27.2 0.7 %copy-start.2 = (f32[128]{0:T(128)S(1)}, f32[128]{0:T(128)}, u32[]{:S(2)}) copy-start(f32[128]{0:T(128)} %param.7) | copy-start | bytes 1540
  41.7 3.1 %copy-start.1 = (f32[2,128]{1,0:T(2,128)}, f32[2,128]{1,0:T(2,128)S(1)}, u32[]{:S(2)}) copy-start(f32[2,128]{1,0:T(2,128)S(1)} %abs_reduce_fusion) | copy-start | bytes 3076
where the time goes:
time: 47.7 us; the launch traced here: 47.4 us
  other arithmetic  20 us (42%)
  waiting for transfers between devices  10.2 us (21%)
  starting transfers between devices  9.58 us (20%)
  local copies, waits for them, and re-layouts  6.85 us (14%)
  between operations  0.73 us (2%)
    all_to_all x1, waiting for transfers between devices, shards(): lax.all_to_all(raw_keys, ('farcp', 'nearcp'), split_axis=0, concat_axis=1...  10.2 us
    sub x1, other arithmetic, turn_pairs(): first * cosine - second * sine  6.33 us
    all_to_all x1, starting transfers between devices, shards(): lax.all_to_all(raw_keys, ('farcp', 'nearcp'), split_axis=0, concat_axis=1...  5.34 us
    mul x1, other arithmetic, unit_rows(): vectors * lax.rsqrt(jnp.mean(vectors * vectors, axis=-1, keepdims=True) +...  4.83 us
    all_to_all x1, starting transfers between devices, shards(): lax.all_to_all(raw_values, ('farcp', 'nearcp'), split_axis=0, concat_axis...  4.24 us
    convert_element_type x1, other arithmetic, shards(): narrow_keys = (turned_keys / key_scale[:, None]).astype(jnp.bfloat16)  3.13 us
    cos x2, local copies, waits for them, and re-layouts, turn_pairs(): jnp.cos(angle)[None, :, None, :]  2.89 us
    unnamed x7, local copies, waits for them, and re-layouts  2.59 us
  transfers between devices with their start and end apart: 2, of which 1 were waited for; matrix products, arithmetic and copies ran while one was open for 51% of the time, Pallas kernels for 0%

commit v1 on v0

v1 whole, which is shorter than its diff:
```python
import jax
import jax.numpy as jnp
from jax import lax
from jax.experimental import pallas as pl
from jax.experimental.pallas import tpu as pltpu
from jax.sharding import PartitionSpec as P

GROUP = ("farcp", "nearcp")


def turn_tables(angle, heads):
    cosine, sine = lax.optimization_barrier((jnp.cos(angle), jnp.sin(angle)))
    length, half = angle.shape
    rows = (length, heads, 2 * half)
    both = jnp.concatenate([cosine, cosine], axis=-1)[:, None, :]
    signed = jnp.concatenate([-sine, sine], axis=-1)[:, None, :]
    return (
        jnp.broadcast_to(both, rows).reshape(length * heads, 2 * half),
        jnp.broadcast_to(signed, rows).reshape(length * heads, 2 * half),
    )


def key_kernel(heads, keys_ref, cos_ref, sin_ref, gain_ref, narrow_ref, scale_ref, turned_ref):
    rows, size = turned_ref.shape
    step = 64 if rows % 64 == 0 else rows
    gain = gain_ref[...]
    group = 8 if (step % 8 == 0 and 8 % heads == 0) else heads

    def turn(i, most):
        at = pl.ds(i * step, step)
        wide = keys_ref[0, at, :].astype(jnp.float32)
        square = jnp.mean(wide * wide, axis=-1, keepdims=True)
        wide = wide * lax.rsqrt(square + 1e-06) * gain
        turned = wide * cos_ref[at, :] + pltpu.roll(wide, size // 2, 1) * sin_ref[at, :]
        turned_ref[at, :] = turned
        return jnp.maximum(most, jnp.max(jnp.abs(turned).reshape(step // group, group, size), axis=0))

    most = lax.fori_loop(0, rows // step, turn, jnp.zeros((group, size), jnp.float32))
    peaks = [
        jnp.max(jnp.concatenate([most[g : g + 1] for g in range(h, group, heads)], axis=0), axis=0, keepdims=True)
        for h in range(heads)
    ]
    scale = jnp.concatenate(peaks, axis=0)
    scale_ref[0] = scale
    inverse = 1.0 / jnp.concatenate([scale] * (group // heads), axis=0)

    def narrow(i, carry):
        at = pl.ds(i * step, step)
        turned = turned_ref[at, :].reshape(step // group, group, size)
        narrow_ref[0, at, :] = (turned * inverse[None]).reshape(step, size).astype(jnp.bfloat16)
        return carry

    lax.fori_loop(0, rows // step, narrow, 0)


def ready_keys(moved_keys, angle, key_gain):
    batch, length, heads, size = moved_keys.shape
    rows = length * heads
    cosine, sine = turn_tables(angle, heads)
    whole = lambda b: (0, 0)
    narrow, scale = pl.pallas_call(
        lambda *refs: key_kernel(heads, *refs),
        grid=(batch,),
        in_specs=[
            pl.BlockSpec((1, rows, size), lambda b: (b, 0, 0)),
            pl.BlockSpec((rows, size), whole),
            pl.BlockSpec((rows, size), whole),
            pl.BlockSpec((1, size), whole),
        ],
        out_specs=[
            pl.BlockSpec((1, rows, size), lambda b: (b, 0, 0)),
            pl.BlockSpec((1, heads, size), lambda b: (b, 0, 0)),
        ],
        out_shape=[
            jax.ShapeDtypeStruct((batch, rows, size), jnp.bfloat16),
            jax.ShapeDtypeStruct((batch, heads, size), jnp.float32),
        ],
        scratch_shapes=[pltpu.VMEM((rows, size), jnp.float32)],
        compiler_params=pltpu.CompilerParams(vmem_limit_bytes=48 * 1024 * 1024),
    )(moved_keys.reshape(batch, rows, size), cosine, sine, key_gain[None])
    return narrow.reshape(batch, length, heads, size), scale


def to_sequences(spread):
    batch, length, heads, size = spread.shape
    members = lax.axis_size(GROUP)
    moved = lax.all_to_all(spread, GROUP, split_axis=0, concat_axis=0, tiled=True)
    if batch != members:
        moved = jnp.swapaxes(moved.reshape(members, batch // members, length, heads, size), 0, 1)
    return moved.reshape(batch // members, length * members, heads, size)


def shards(raw_keys, raw_values, turn_angle, key_gain):
    moved_keys = to_sequences(raw_keys)
    cache_values = to_sequences(raw_values)
    narrow_keys, key_scale = ready_keys(moved_keys, turn_angle, key_gain)
    return (narrow_keys, cache_values, key_scale)


def solution(mesh):
    in_specs = (
        P(None, GROUP, "heads", None),
        P(None, GROUP, "heads", None),
        P(),
        P(),
    )
    out_specs = (
        P(GROUP, None, "heads", None),
        P(GROUP, None, "heads", None),
        P(GROUP, "heads", None),
    )
    return jax.shard_map(shards, mesh=mesh, in_specs=in_specs, out_specs=out_specs, check_vma=False)
```

time: 47.7 us -> 53.7 us (1.13)
  blocking collectives: 0 us -> 19.9 us
  other arithmetic: 20 us -> 1.26 us
  Pallas kernels: 0 us -> 12.4 us
  starting transfers between devices: 9.58 us -> 3.56 us
  waiting for transfers between devices: 10.2 us -> 9.41 us
  local copies, waits for them, and re-layouts: 6.85 us -> 6.23 us
    all_to_all x0 -> x1, blocking collectives: none -> 19.9 us  [to_sequences(): lax.all_to_all(spread, GROUP, split_axis=0, concat_axis=0, tiled=True)]
    pallas_call x0 -> x1, Pallas kernels: none -> 12.4 us  [ready_keys(): pl.pallas_call(lambda *refs: key_kernel(heads, *refs), grid=(batch,), in_...]
    sub x1 -> x0, other arithmetic: 6.33 us -> none  [turn_pairs(): first * cosine - second * sine]
    all_to_all x2 -> x1, starting transfers between devices: 9.58 us -> 3.56 us  [to_sequences(): lax.all_to_all(spread, GROUP, split_axis=0, concat_axis=0, tiled=True)]
    mul x1 -> x0, other arithmetic: 4.83 us -> none  [unit_rows(): vectors * lax.rsqrt(jnp.mean(vectors * vectors, axis=-1, keepdims=True) +...]
    convert_element_type x2 -> x0, other arithmetic: 3.85 us -> none  [the longest x1 3.13 us: shards(): narrow_keys = (turned_keys / key_scale[:, None]).astype(jnp.bfloat16)]
    cos x2 -> x0, local copies, waits for them, and re-layouts: 2.89 us -> none  [turn_pairs(): jnp.cos(angle)[None, :, None, :]]
    reduce_max x1 -> x0, other arithmetic: 2.55 us -> none  [shards(): key_scale = jnp.max(jnp.abs(turned_keys), axis=1)]
  transfers between devices with their start and end apart: 2 -> 1, of which waited for: 1 -> 1; matrix products, arithmetic and copies ran while one was open for 51% -> 9% of each run, Pallas kernels for 0% -> 0%
where the time goes in v1:
time: 53.7 us; the launch traced here: 53.5 us
  blocking collectives  19.9 us (37%)
  Pallas kernels  12.4 us (23%)
  waiting for transfers between devices  9.41 us (18%)
  local copies, waits for them, and re-layouts  6.23 us (12%)
  starting transfers between devices  3.56 us (7%)
  other arithmetic  1.26 us (2%)
  between operations  0.73 us (1%)
    all_to_all x1, blocking collectives, to_sequences(): lax.all_to_all(spread, GROUP, split_axis=0, concat_axis=0, tiled=True)  19.9 us
    pallas_call x1, Pallas kernels, ready_keys(): pl.pallas_call(lambda *refs: key_kernel(heads, *refs), grid=(batch,), in_...  12.4 us
    all_to_all x1, waiting for transfers between devices, to_sequences(): lax.all_to_all(spread, GROUP, split_axis=0, concat_axis=0, tiled=True)  9.41 us
    all_to_all x1, starting transfers between devices, to_sequences(): lax.all_to_all(spread, GROUP, split_axis=0, concat_axis=0, tiled=True)  3.56 us
    sin x1, local copies, waits for them, and re-layouts, turn_tables(): cosine, sine = lax.optimization_barrier((jnp.cos(angle), jnp.sin(angle)))  1.86 us
    concatenate x1, local copies, waits for them, and re-layouts, turn_tables(): signed = jnp.concatenate([-sine, sine], axis=-1)[:, None, :]  1.55 us
    concatenate x1, other arithmetic, turn_tables(): both = jnp.concatenate([cosine, cosine], axis=-1)[:, None, :]  1.22 us
  transfers between devices with their start and end apart: 1, of which 1 were waited for; matrix products, arithmetic and copies ran while one was open for 9% of the time, Pallas kernels for 0%

profile of v1, /device:TPU:0, one launch (start us, length us, event | category | flops | bytes accessed | tf_op | source)
XLA Modules:
  0.0 53.5 jit_solution(7129892558858555645)
XLA Ops:
  0.6 0.0 copy-start.2
  0.6 19.9 %all_to_all.10 = bf16[8,256,2,128]{3,2,1,0:T(2,128)(2,1)} all-to-all(bf16[8,256,2,128]{3,2,1,0:T(2,128)(2,1)} %param.5), channel_id=1, replica_groups=mesh['farcp'=4,'nearcp'=2,'heads'=4] {'farcp','nearcp'}, dimensions={0} | all-to-all | bytes 2097152 | tf_op jit(solution)/shard_map/all_to_all | solution.py:87
  20.5 3.6 %all-to-all-start = ((bf16[8,256,2,128]{3,2,1,0:T(2,128)(2,1)}), bf16[8,256,2,128]{3,2,1,0:T(2,128)(2,1)S(1)}, u32[]{:S(2)}, u32[]{:S(2)}) async-start(bf16[8,256,2,128]{3,2,1,0:T(2,128)(2,1)} %param.4), calls=%async_computation | async-start | bytes 2097152 | tf_op jit(solution)/shard_map/all_to_all | solution.py:87
  24.1 0.0 copy-done.2
  24.1 1.9 %fusion = (f32[2048,64]{0,1:T(8,128)S(1)}, f32[2048,64]{0,1:T(8,128)S(1)}) fusion(f32[2048,64]{0,1:T(8,128)S(1)} %copy-done.2), kind=kLoop, calls=%fused_computation.2 | loop fusion | bytes 1572864 | tf_op jit(solution)/shard_map/sin | solution.py:12
  26.0 1.2 %pad_maximum_fusion = (f32[2048,128]{0,1:T(8,128)S(1)}, f32[2048,128]{0,1:T(8,128)}) fusion(f32[2048,64]{0,1:T(8,128)S(1)} %get-tuple-element.7, f32[2048,64]{0,1:T(8,128)S(1)} %get-tuple-element.8, f32[2048,64]{0,1:T(8,128)S(1)} %neg.3), kind=kLoop, calls=%fused_computation | loop fusion | flops 524288 | bytes 3670016 | tf_op jit(solution)/shard_map/concatenate | solution.py:15
  27.2 0.3 copy.7
  27.6 1.6 %copy.8 = f32[2048,128]{1,0:T(8,128)S(1)} copy(f32[2048,128]{0,1:T(8,128)} %get-tuple-element.14) | data formatting | bytes 2097152 | tf_op jit(solution)/shard_map/concatenate | solution.py:16
  29.1 9.4 %all-to-all-done = bf16[8,256,2,128]{3,2,1,0:T(2,128)(2,1)S(1)} async-done(((bf16[8,256,2,128]{3,2,1,0:T(2,128)(2,1)}), bf16[8,256,2,128]{3,2,1,0:T(2,128)(2,1)S(1)}, u32[]{:S(2)}, u32[]{:S(2)}) %all-to-all-start) | async-done | bytes 1048608 | tf_op jit(solution)/shard_map/all_to_all | solution.py:87
  38.5 0.7 %broadcast_in_dim.6 = f32[2048,2,128]{2,1,0:T(2,128)S(1)} broadcast(f32[2048,128]{1,0:T(8,128)S(1)} %copy.7), dimensions={0,2} | broadcast | bytes 3145728 | tf_op jit(solution)/shard_map/broadcast_in_dim | solution.py:18
  39.3 0.0 copy-start
  39.3 0.8 %broadcast_in_dim.7 = f32[2048,2,128]{2,1,0:T(2,128)S(1)} broadcast(f32[2048,128]{1,0:T(8,128)S(1)} %copy.8), dimensions={0,2} | broadcast | bytes 3145728 | tf_op jit(solution)/shard_map/broadcast_in_dim | solution.py:19
  40.1 0.0 copy-done
  40.1 0.0 copy-start.1
  40.1 12.4 %shard_map.67 = (bf16[1,4096,128]{2,1,0:T(8,128)(2,1)}, f32[1,2,128]{2,1,0:T(2,128)}) custom-call(bf16[1,4096,128]{2,1,0:T(8,128)(2,1)S(1)} %bitcast.8, f32[4096,128]{1,0:T(8,128)S(1)} %bitcast.6, f32[4096,128]{1,0:T(8,128)S(1)} %bitcast.7, f32[1,128]{1,0:T(1,128)S(1)} %bitcast.9), custom_call_target="tpu_custom_call" | custom-call | tf_op jit(solution)/shard_map/pallas_call | solution.py:61
  52.5 0.0 copy-done.1
  52.5 1.0 %copy.10 = bf16[1,2048,2,128]{3,2,1,0:T(2,128)(2,1)} copy(bf16[1,2048,2,128]{3,2,1,0:T(2,128)(2,1)S(1)} %bitcast.10) | data formatting | bytes 2097152
  (1 shorter events, 0.0 us)
Async XLA Ops:
  0.6 23.5 %copy-start.2 = (f32[2048,64]{0,1:T(8,128)S(1)}, f32[2048,64]{0,1:T(8,128)}, u32[]{:S(2)}) copy-start(f32[2048,64]{0,1:T(8,128)} %param.6) | copy-start | bytes 1572868
  20.5 18.0 %all-to-all-start = ((bf16[8,256,2,128]{3,2,1,0:T(2,128)(2,1)}), bf16[8,256,2,128]{3,2,1,0:T(2,128)(2,1)S(1)}, u32[]{:S(2)}, u32[]{:S(2)}) async-start(bf16[8,256,2,128]{3,2,1,0:T(2,128)(2,1)} %param.4), calls=%async_computation | async-start | bytes 2097152 | tf_op jit(solution)/shard_map/all_to_all | solution.py:87
  39.3 0.8 %copy-start = (f32[128]{0:T(128)S(1)}, f32[128]{0:T(128)}, u32[]{:S(2)}) copy-start(f32[128]{0:T(128)} %param.7) | copy-start | bytes 1540
  40.1 12.4 %copy-start.1 = (bf16[8,256,2,128]{3,2,1,0:T(2,128)(2,1)S(1)}, bf16[8,256,2,128]{3,2,1,0:T(2,128)(2,1)}, u32[]{:S(2)}) copy-start(bf16[8,256,2,128]{3,2,1,0:T(2,128)(2,1)} %all_to_all.10) | copy-start | bytes 3145732
